TPU v7x, 32 devices: a whole 2x2x4 slice. The times are simulated.
32 devices in a mesh: pp: 4 (over z), tp: 4 (over y, core), ep: 2 (over x).
Axes of the slice: x: 2, y: 2, z: 4, core: 2. Of those that a mesh axis runs over, the one named last changes fastest.
Arguments:
- incoming: bfloat16 [4, 1024, 2048], P('pp', ('tp', 'ep')), may hold values from -6 to 6
- expert_ids: int32 [4, 1024, 2], P('pp', ('tp', 'ep')), may hold values from 0 to 7, all different within a row; in each aligned block of 128 rows (0 to 127, 128 to 255, ..., all dimensions but the last counted through in order) at most 64 rows name the same one
- gate_scores: float32 [4, 1024, 2], P('pp', ('tp', 'ep')), may hold values from 0.05 to 1
- gate_proj: bfloat16 [8, 2048, 768], P(('tp', 'ep')), may hold values from -0.125 to 0.125
- up_proj: bfloat16 [8, 2048, 768], P(('tp', 'ep')), may hold values from -0.125 to 0.125
- down_proj: bfloat16 [8, 768, 2048], P(('tp', 'ep')), may hold values from -0.21875 to 0.21875
Outputs:
- combined: bfloat16 [4, 1024, 2048], P('pp', ('tp', 'ep'))
Inputs may be any that keep to these rules, and one draw needn't show every extreme that they name: `expert_ids`: each token names 2 different experts. Among the tokens of one device of one section no expert is named more than 64 times, and in every draw some device's tokens name one expert exactly 64 times.
All inputs are finite; a program needn't handle non-finite values.
Results may differ from a plain program's by a relative error of at most 0.0045.
Values may be sent and summed in bfloat16 or wider, within the bound.
A program may use at most 64 MiB of HBM per device.

v0:
```python
import jax
import jax.numpy as jnp
from jax import lax
from jax.sharding import PartitionSpec as P


def shifted(block, axis, distance):
    devices = range(lax.axis_size(axis))
    route = [((i - distance) % len(devices), i) for i in devices]
    return lax.ppermute(block, axis, route)


def expert_apply(tokens_in, gate_mat, up_mat, down_mat):
    gate_part = jnp.dot(tokens_in, gate_mat, preferred_element_type=jnp.float32)
    upward = jnp.dot(tokens_in, up_mat, preferred_element_type=jnp.float32)
    hidden = (jax.nn.silu(gate_part) * upward).astype(jnp.bfloat16)
    return jnp.dot(hidden, down_mat, preferred_element_type=jnp.float32).astype(jnp.bfloat16)


def shards(incoming, expert_ids, gate_scores, gate_proj, up_proj, down_proj):
    arrived = shifted(incoming, "pp", 1)[0]
    tok_count, features = arrived.shape
    top_count = expert_ids.shape[2]
    expert_count = lax.axis_size("tp") * lax.axis_size("ep")
    capacity = min(tok_count, 2 * tok_count * top_count // expert_count)
    values = arrived.astype(jnp.float32)
    normed = (values * lax.rsqrt(jnp.mean(values * values, axis=1, keepdims=True) + 1e-06)).astype(
        jnp.bfloat16
    )
    chosen = expert_ids[0].reshape(-1)
    onehot = (chosen[:, None] == jnp.arange(expert_count, dtype=jnp.int32)[None, :]).astype(
        jnp.int32
    )
    before = jnp.cumsum(onehot, axis=0) - onehot
    slot_of = jnp.sum(before * onehot, axis=1)
    destination = chosen * capacity + slot_of
    owner_row = jnp.arange(chosen.shape[0], dtype=jnp.int32) // top_count
    source_row = (
        jnp.full((expert_count * capacity,), tok_count, jnp.int32).at[destination].set(owner_row)
    )
    occupied = jnp.zeros((expert_count * capacity,), jnp.int32).at[destination].set(1)
    with_blank = jnp.concatenate([normed, jnp.zeros((1, features), jnp.bfloat16)], axis=0)
    outgoing = with_blank[source_row].reshape(expert_count, capacity, features)
    occupied = occupied.reshape(expert_count, capacity)
    gate_mat, up_mat, down_mat = (gate_proj[0], up_proj[0], down_proj[0])
    received_rows = lax.all_to_all(outgoing, ("tp", "ep"), split_axis=0, concat_axis=0, tiled=True)
    flat_rows = received_rows.reshape(-1, features)
    flat_live = lax.all_to_all(
        occupied, ("tp", "ep"), split_axis=0, concat_axis=0, tiled=True
    ).reshape(-1)
    answered = expert_apply(flat_rows, gate_mat, up_mat, down_mat) * flat_live[:, None].astype(
        jnp.bfloat16
    )
    answered = answered.reshape(received_rows.shape)
    returned = lax.all_to_all(answered, ("tp", "ep"), split_axis=0, concat_axis=0, tiled=True)
    picked = returned.reshape(expert_count * capacity, features)[destination].reshape(
        tok_count, top_count, features
    )
    scores = gate_scores[0]
    weights = scores / jnp.sum(scores, axis=1, keepdims=True)
    combined = values + jnp.sum(weights[:, :, None] * picked.astype(jnp.float32), axis=1)
    return combined.astype(jnp.bfloat16)[None]


def solution(mesh):
    placed = (
        P("pp", ("tp", "ep"), None),
        P("pp", ("tp", "ep"), None),
        P("pp", ("tp", "ep"), None),
        P(("tp", "ep"), None, None),
        P(("tp", "ep"), None, None),
        P(("tp", "ep"), None, None),
    )
    return jax.shard_map(
        shards, mesh=mesh, in_specs=placed, out_specs=P("pp", ("tp", "ep"), None), check_vma=False
    )
```

profile of v0, /device:TPU:0, one launch (start us, length us, event | category | flops | bytes accessed | tf_op | source)
XLA Modules:
  0.0 117.0 jit_solution(36195147983745656)
XLA Ops:
  0.0 3.1 %collective-permute-start = (bf16[1,128,2048]{2,1,0:T(8,128)(2,1)}, bf16[1,128,2048]{2,1,0:T(8,128)(2,1)}, u32[]{:S(2)}, u32[]{:S(2)}) collective-permute-start(bf16[1,128,2048]{2,1,0:T(8,128)(2,1)} %param.6), channel_id=1, source_target_pairs={{24,0},{0,8},{8,16},{16,24},{25,1},{1,9},{9,17},{17,25},{26,2},{2,... | collective-permute-start | bytes 1572872 | tf_op jit(solution)/shard_map/ppermute | solution.py:10
  3.1 0.8 copy.14
  4.1 0.7 broadcast_multiply_fusion
  4.8 0.6 reduce-window.6
  5.4 0.2 slice_reduce_fusion
  6.0 1.4 %scatter_custom_fusion.1 = s32[512]{0:T(512)S(1)} fusion(s32[256]{0:T(256)S(1)} %bitcast.49, s32[256]{0:T(256)S(1)} %ne.14, s32[]{:T(128)} %constant.38.clone.1), kind=kCustom, calls=%fused_computation.38 | custom fusion | bytes 2052 | tf_op jit(solution)/shard_map/scatter | solution.py:41
  7.4 0.7 all_to_all.13
  8.1 3.7 %all-to-all-start.1 = ((s32[8,1,64]{2,1,0:T(1,128)}), s32[8,1,64]{2,1,0:T(1,128)S(1)}, u32[]{:S(2)}, u32[]{:S(2)}) async-start(s32[8,1,64]{2,1,0:T(1,128)} %all_to_all.13), calls=%async_computation.1 | async-start | bytes 8192 | tf_op jit(solution)/shard_map/all_to_all | solution.py:48
  11.8 1.4 %scatter_custom_fusion = s32[512]{0:T(512)S(1)} fusion(s32[256]{0:T(256)S(1)} %bitcast.50, s32[256]{0:T(256)S(1)} %and_select_fusion, s32[]{:T(128)} %constant.36.clone.1), kind=kCustom, calls=%fused_computation.40 | custom fusion | bytes 2052 | tf_op jit(solution)/shard_map/scatter | solution.py:39
  13.2 4.1 %collective-permute-done = bf16[1,128,2048]{2,1,0:T(8,128)(2,1)} collective-permute-done((bf16[1,128,2048]{2,1,0:T(8,128)(2,1)}, bf16[1,128,2048]{2,1,0:T(8,128)(2,1)}, u32[]{:S(2)}, u32[]{:S(2)}) %collective-permute-start) | collective-permute-done | bytes 524320 | tf_op jit(solution)/shard_map/ppermute | solution.py:10
  17.3 1.2 %fusion.16 = f32[128]{0:T(128)S(1)} fusion(bf16[1,128,2048]{2,1,0:T(8,128)(2,1)} %collective-permute-done), kind=kLoop, calls=%fused_computation.18 | loop fusion | flops 786304 | bytes 524800 | tf_op jit(solution)/shard_map/reduce_sum | solution.py:27
  18.6 1.2 %fusion.17 = bf16[128,2048]{1,0:T(8,128)(2,1)S(1)} fusion(bf16[1,128,2048]{2,1,0:T(8,128)(2,1)} %collective-permute-done, f32[128]{0:T(128)S(1)} %add_rsqrt_fusion), kind=kLoop, calls=%fused_computation.19 | loop fusion | flops 786432 | bytes 1049088 | tf_op jit(solution)/shard_map/convert_element_type | solution.py:27
  19.8 0.8 concatenate.3
  20.6 6.4 %gather_fusion = bf16[512,2048]{1,0:T(8,128)(2,1)} fusion(bf16[129,2048]{1,0:T(8,128)(2,1)} %concatenate.3, s32[1024]{0:T(1024)S(1)} %pad_clamp_fusion.1), kind=kCustom, calls=%fused_computation | custom fusion | bytes 4196352 | tf_op jit(solution)/shard_map/gather | solution.py:43
  27.0 4.3 %all-to-all-start = ((bf16[8,64,2048]{2,1,0:T(8,128)(2,1)}), bf16[8,64,2048]{2,1,0:T(8,128)(2,1)}, u32[]{:S(2)}, u32[]{:S(2)}) async-start(bf16[8,64,2048]{2,1,0:T(8,128)(2,1)} %bitcast.47), calls=%async_computation | async-start | bytes 4194304 | tf_op jit(solution)/shard_map/all_to_all | solution.py:46
  31.4 25.9 %all-to-all-done = bf16[8,64,2048]{2,1,0:T(8,128)(2,1)} async-done(((bf16[8,64,2048]{2,1,0:T(8,128)(2,1)}), bf16[8,64,2048]{2,1,0:T(8,128)(2,1)}, u32[]{:S(2)}, u32[]{:S(2)}) %all-to-all-start) | async-done | bytes 2097184 | tf_op jit(solution)/shard_map/all_to_all | solution.py:46
  57.4 5.5 %fusion.4 = f32[512,768]{1,0:T(8,128)} fusion(bf16[512,2048]{1,0:T(8,128)(2,1)} %bitcast.7, bf16[1,2048,768]{2,1,0:T(8,128)(2,1)} %param.9), kind=kOutput, calls=%fused_computation.8 | convolution fusion | flops 1610612736 | bytes 6815744 | tf_op jit(solution)/shard_map/dot_general | solution.py:14
  62.9 8.2 %fusion.9 = bf16[512,2048]{1,0:T(8,128)(2,1)} fusion(bf16[1,768,2048]{2,1,0:T(8,128)(2,1)S(1)} %copy-done, bf16[512]{0:T(512)(128)(2,1)S(1)} %convert_element_type.55, f32[512,768]{1,0:T(8,128)} %fusion.4, bf16[512,2048]{1,0:T(8,128)(2,1)} %bitcast.7, bf16[1,2048,768]{2,1,0:T(8,128)(2,1)} %param.10), kind=kOutput, calls=%fused_computation.11 | convolution fusion | flops 3228827648 | bytes 12059648 | tf_op jit(solution)/shard_map/dot_general | solution.py:17
  71.1 4.7 %all-to-all-start.2 = ((bf16[8,64,2048]{2,1,0:T(8,128)(2,1)}), bf16[8,64,2048]{2,1,0:T(8,128)(2,1)}, u32[]{:S(2)}, u32[]{:S(2)}) async-start(bf16[8,64,2048]{2,1,0:T(8,128)(2,1)} %bitcast.48), calls=%async_computation.2 | async-start | bytes 4194304 | tf_op jit(solution)/shard_map/all_to_all | solution.py:55
  75.9 25.7 %all-to-all-done.2 = bf16[8,64,2048]{2,1,0:T(8,128)(2,1)} async-done(((bf16[8,64,2048]{2,1,0:T(8,128)(2,1)}), bf16[8,64,2048]{2,1,0:T(8,128)(2,1)}, u32[]{:S(2)}, u32[]{:S(2)}) %all-to-all-start.2) | async-done | bytes 2097184 | tf_op jit(solution)/shard_map/all_to_all | solution.py:55
  101.6 5.2 %gather_fusion.1 = bf16[256,2048]{1,0:T(8,128)(2,1)} fusion(bf16[512,2048]{1,0:T(8,128)(2,1)} %bitcast.12, s32[1024]{0:T(1024)S(1)} %pad_clamp_fusion), kind=kCustom, calls=%fused_computation.1 | custom fusion | bytes 2098176 | tf_op jit(solution)/shard_map/gather | solution.py:56
  106.8 3.4 %reshape.110 = f32[128,2,2048]{2,1,0:T(2,128)} reshape(bf16[256,2048]{1,0:T(8,128)(2,1)} %gather_fusion.1) | data formatting | bytes 3145728 | tf_op jit(solution)/shard_map/convert_element_type | solution.py:61
  110.2 4.8 %multiply_reduce_fusion = f32[128,2048]{1,0:T(8,128)S(1)} fusion(f32[128,2,2048]{2,1,0:T(2,128)} %reshape.110, f32[128,2]{1,0:T(8,128)S(1)} %copy.12), kind=kLoop, calls=%fused_computation.12 | loop fusion | flops 786432 | bytes 3146752 | tf_op jit(solution)/shard_map/reduce_sum | solution.py:61
  115.0 2.0 %fusion.18 = bf16[1,128,2048]{2,1,0:T(8,128)(2,1)} fusion(bf16[1,128,2048]{2,1,0:T(8,128)(2,1)} %collective-permute-done, f32[128,2048]{1,0:T(8,128)S(1)} %multiply_reduce_fusion), kind=kLoop, calls=%fused_computation.20 | loop fusion | flops 786432 | bytes 2097152 | tf_op jit(solution)/shard_map/convert_element_type | solution.py:62
  (25 shorter events, 1.0 us)
Async XLA Ops:
  0.0 62.9 %copy-start = (bf16[1,768,2048]{2,1,0:T(8,128)(2,1)S(1)}, bf16[1,768,2048]{2,1,0:T(8,128)(2,1)}, u32[]{:S(2)}) copy-start(bf16[1,768,2048]{2,1,0:T(8,128)(2,1)} %param.11) | copy-start | bytes 9437188
  0.0 17.3 %collective-permute-start = (bf16[1,128,2048]{2,1,0:T(8,128)(2,1)}, bf16[1,128,2048]{2,1,0:T(8,128)(2,1)}, u32[]{:S(2)}, u32[]{:S(2)}) collective-permute-start(bf16[1,128,2048]{2,1,0:T(8,128)(2,1)} %param.6), channel_id=1, source_target_pairs={{24,0},{0,8},{8,16},{16,24},{25,1},{1,9},{9,17},{17,25},{26,2},{2,... | collective-permute-start | bytes 1572872 | tf_op jit(solution)/shard_map/ppermute | solution.py:10
  8.1 18.9 %all-to-all-start.1 = ((s32[8,1,64]{2,1,0:T(1,128)}), s32[8,1,64]{2,1,0:T(1,128)S(1)}, u32[]{:S(2)}, u32[]{:S(2)}) async-start(s32[8,1,64]{2,1,0:T(1,128)} %all_to_all.13), calls=%async_computation.1 | async-start | bytes 8192 | tf_op jit(solution)/shard_map/all_to_all | solution.py:48
  27.0 30.4 %all-to-all-start = ((bf16[8,64,2048]{2,1,0:T(8,128)(2,1)}), bf16[8,64,2048]{2,1,0:T(8,128)(2,1)}, u32[]{:S(2)}, u32[]{:S(2)}) async-start(bf16[8,64,2048]{2,1,0:T(8,128)(2,1)} %bitcast.47), calls=%async_computation | async-start | bytes 4194304 | tf_op jit(solution)/shard_map/all_to_all | solution.py:46
  71.1 4.7 %copy-start.1 = (f32[1,128,2]{1,2,0:T(2,128)S(1)}, f32[1,128,2]{1,2,0:T(2,128)}, u32[]{:S(2)}) copy-start(f32[1,128,2]{1,2,0:T(2,128)} %param.8) | copy-start | bytes 3076
  71.1 30.5 %all-to-all-start.2 = ((bf16[8,64,2048]{2,1,0:T(8,128)(2,1)}), bf16[8,64,2048]{2,1,0:T(8,128)(2,1)}, u32[]{:S(2)}, u32[]{:S(2)}) async-start(bf16[8,64,2048]{2,1,0:T(8,128)(2,1)} %bitcast.48), calls=%async_computation.2 | async-start | bytes 4194304 | tf_op jit(solution)/shard_map/all_to_all | solution.py:55
where the time goes:
time: 118 us; the launch traced here: 117 us
  waiting for transfers between devices  55.7 us (47%)
  local copies, waits for them, and re-layouts  21 us (18%)
  starting transfers between devices  15.8 us (13%)
  matrix products  13.7 us (12%)
  other arithmetic  10.7 us (9%)
    all_to_all x1, waiting for transfers between devices, shards(): lax.all_to_all(outgoing, ('tp', 'ep'), split_axis=0, concat_axis=0, tiled...  25.9 us
    all_to_all x1, waiting for transfers between devices, shards(): lax.all_to_all(answered, ('tp', 'ep'), split_axis=0, concat_axis=0, tiled...  25.7 us
    dot_general x1, matrix products, expert_apply(): jnp.dot(hidden, down_mat, preferred_element_type=jnp.float32)  8.23 us
    gather x1, local copies, waits for them, and re-layouts, shards(): outgoing = with_blank[source_row].reshape(expert_count, capacity, features)  6.36 us
    dot_general x1, matrix products, expert_apply(): gate_part = jnp.dot(tokens_in, gate_mat, preferred_element_type=jnp.float32)  5.48 us
    gather x1, local copies, waits for them, and re-layouts, shards(): returned.reshape(expert_count * capacity, features)[destination]  5.21 us
    reduce_sum x1, other arithmetic, shards(): jnp.sum(weights[:, :, None] * picked.astype(jnp.float32), axis=1)  4.81 us
    all_to_all x1, starting transfers between devices, shards(): lax.all_to_all(answered, ('tp', 'ep'), split_axis=0, concat_axis=0, tiled...  4.65 us
  transfers between devices with their start and end apart: 4, of which 3 were waited for; matrix products, arithmetic and copies ran while one was open for 13% of the time, Pallas kernels for 0%

commit v1 on v0

--- a/solution.py
+++ b/solution.py
@@ -1,7 +1,14 @@
+import functools
+
 import jax
 import jax.numpy as jnp
 from jax import lax
+from jax.experimental import pallas as pl
+from jax.experimental.pallas import tpu as pltpu
 from jax.sharding import PartitionSpec as P
+
+MESH = pl.DeviceIdType.MESH
+OWN, ACROSS_X, ACROSS_Y, DIAGONAL = range(4)
 
 
 def shifted(block, axis, distance):
@@ -62,6 +69,320 @@
     return combined.astype(jnp.bfloat16)[None]
 
 
+def exchange_kernel(
+    sizes,
+    incoming,
+    routing,
+    gate_hbm,
+    up_hbm,
+    down_hbm,
+    out_ref,
+    gate_w,
+    up_w,
+    down_w,
+    tok,
+    meta,
+    packed,
+    hidden,
+    kept,
+    passed,
+    partner,
+    to_x,
+    to_y,
+    to_d,
+    from_x,
+    from_y,
+    via_x,
+    via_y,
+    total,
+    send_sem,
+    recv_sem,
+    load_sem,
+):
+    n_pp, n_tp, n_ep, top, cap, chunks, pieces = sizes
+    rows, features = tok.shape[2:]
+    ff = hidden.shape[1]
+    pp, tp, ep = lax.axis_index("pp"), lax.axis_index("tp"), lax.axis_index("ep")
+    other_core = tp + 1 - 2 * (tp % 2)
+    at_x = {"ep": (ep + 1) % n_ep}
+    at_y = {"tp": (tp + 2) % n_tp}
+    at_core = {"tp": other_core}
+    ahead, behind = {"pp": (pp + 1) % n_pp}, {"pp": (pp + n_pp - 1) % n_pp}
+
+    loads = [
+        pltpu.make_async_copy(src.at[0], dst, load_sem.at[i])
+        for i, (src, dst) in enumerate(((gate_hbm, gate_w), (up_hbm, up_w), (down_hbm, down_w)))
+    ]
+    own_meta = pltpu.make_async_copy(routing, meta.at[0], load_sem.at[3])
+
+    barrier = pltpu.get_barrier_semaphore()
+    for peer in (at_x, at_y, at_core, ahead, behind):
+        pl.semaphore_signal(barrier, inc=1, device_id=peer, device_id_type=MESH)
+    own_meta.start()
+    pl.semaphore_wait(barrier, 5)
+
+    started = []
+
+    def link(src, dst, peer):
+        i = len(started)
+        copy = pltpu.make_async_remote_copy(
+            src_ref=src,
+            dst_ref=dst,
+            send_sem=send_sem.at[i],
+            recv_sem=recv_sem.at[i],
+            device_id=peer,
+            device_id_type=MESH,
+        )
+        started.append(copy)
+        copy.start()
+        return copy
+
+    size = rows // chunks
+    part = [pl.ds(c * size, size) for c in range(chunks)]
+
+    def block(role, side, c):
+        return tok.at[role, side, part[c]]
+
+    hop = [link(incoming.at[0, part[c]], block(OWN, 0, c), ahead) for c in range(chunks)]
+    for copy in loads:
+        copy.start()
+    own_meta.wait()
+    meta_x = link(meta.at[0], meta.at[2], at_x)
+    meta_y = link(meta.at[0], meta.at[4], at_y)
+    meta_core = [link(meta.at[0], meta.at[1], at_core)]
+    out_x, out_y, out_d, core = {}, {}, {}, {}
+
+    def relay(c):
+        out_x[c].wait_recv()
+        if c % 2 == 0:
+            out_d[c] = link(block(ACROSS_X, 0, c), block(DIAGONAL, 0, c), at_y)
+        core[ACROSS_X, c] = link(block(ACROSS_X, 0, c), block(ACROSS_X, 1, c), at_core)
+        out_y[c].wait_recv()
+        if c % 2 == 1:
+            out_d[c] = link(block(ACROSS_Y, 0, c), block(DIAGONAL, 0, c), at_x)
+        core[ACROSS_Y, c] = link(block(ACROSS_Y, 0, c), block(ACROSS_Y, 1, c), at_core)
+
+    def relay_diagonal(c):
+        out_d[c].wait_recv()
+        core[DIAGONAL, c] = link(block(DIAGONAL, 0, c), block(DIAGONAL, 1, c), at_core)
+
+    lag = 2
+    for c in range(chunks):
+        hop[c].wait_recv()
+        out_x[c] = link(block(OWN, 0, c), block(ACROSS_X, 0, c), at_x)
+        out_y[c] = link(block(OWN, 0, c), block(ACROSS_Y, 0, c), at_y)
+        core[OWN, c] = link(block(OWN, 0, c), block(OWN, 1, c), at_core)
+        if c == 0:
+            meta_x.wait_recv()
+            meta_d = link(meta.at[2], meta.at[6], at_y)
+            meta_core.append(link(meta.at[2], meta.at[3], at_core))
+            meta_y.wait_recv()
+            meta_core.append(link(meta.at[4], meta.at[5], at_core))
+        if c == 1:
+            meta_d.wait_recv()
+            meta_core.append(link(meta.at[6], meta.at[7], at_core))
+        if c >= lag:
+            relay(c - lag)
+    for copy in meta_core:
+        copy.wait_recv()
+
+    lane = lax.broadcasted_iota(jnp.int32, (rows, rows), 1)
+    earlier = (lax.broadcasted_iota(jnp.int32, (rows, rows), 0) < lane).astype(jnp.bfloat16)
+    ids = [meta[:, k, :] for k in range(top)]
+    scores = [meta[:, top + k, :] for k in range(top)]
+    score_sum = functools.reduce(jnp.add, scores)
+
+    def ranks(expert):
+        named = [i == expert for i in ids]
+        any_named = functools.reduce(jnp.logical_or, named)
+        before = jnp.dot(
+            any_named.astype(jnp.float32).astype(jnp.bfloat16),
+            earlier,
+            preferred_element_type=jnp.float32,
+        )
+        score = sum(jnp.where(n, s, 0.0) for n, s in zip(named, scores))
+        return jnp.where(any_named, before, -1.0), score / score_sum
+
+    mine = (tp * n_ep + ep).astype(jnp.float32)
+    theirs = (other_core * n_ep + ep).astype(jnp.float32)
+    slot_mine, weight_mine = ranks(mine)
+    slot_theirs, _ = ranks(theirs)
+    slot_index = lax.broadcasted_iota(jnp.int32, (cap, rows), 0).astype(jnp.float32)
+
+    def slots(rank, i):
+        return slot_index == rank[i : i + 1, :]
+
+    def pack(role):
+        for side in range(2):
+            pick = slots(slot_mine, 2 * role + side)
+            chosen = jnp.dot(
+                pick.astype(jnp.float32).astype(jnp.bfloat16),
+                tok[role, side],
+                preferred_element_type=jnp.float32,
+            )
+            scale = lax.rsqrt(jnp.mean(chosen * chosen, axis=1, keepdims=True) + 1e-06)
+            packed[role, pl.ds(side * cap, cap)] = (chosen * scale).astype(jnp.bfloat16)
+
+    def expert(role):
+        step = 256 if ff % 256 == 0 else 128
+        tokens_in = packed[role]
+        for n in range(ff // step):
+            cols = pl.ds(n * step, step)
+            gate = jnp.dot(tokens_in, gate_w[:, cols], preferred_element_type=jnp.float32)
+            upward = jnp.dot(tokens_in, up_w[:, cols], preferred_element_type=jnp.float32)
+            hidden[:, cols] = (gate / (1.0 + jnp.exp(-gate)) * upward).astype(jnp.bfloat16)
+        weight = [
+            jnp.sum(
+                jnp.where(slots(slot_mine, 2 * role + side), weight_mine[2 * role + side :][:1], 0.0),
+                axis=1,
+                keepdims=True,
+            )
+            for side in range(2)
+        ]
+        inner = hidden[...]
+        for n in range(features // 256):
+            cols = pl.ds(n * 256, 256)
+            y = jnp.dot(inner, down_w[:, cols], preferred_element_type=jnp.float32)
+            y = y.astype(jnp.bfloat16).astype(jnp.float32)
+            kept[role, :, cols] = (y[:cap] * weight[0]).astype(jnp.bfloat16)
+            passed[role, :, cols] = (y[cap:] * weight[1]).astype(jnp.bfloat16)
+        return link(passed.at[role], partner.at[role], at_core)
+
+    def spread(role):
+        both = jnp.concatenate(
+            [slots(slot_mine, 2 * role), slots(slot_theirs, 2 * role)], axis=0
+        ).astype(jnp.float32)
+        return both.T.astype(jnp.bfloat16)
+
+    def unpack(role, matrix, lo, hi):
+        values = jnp.concatenate([kept[role], partner[role]], axis=0)
+        return jnp.dot(matrix[lo:hi], values, preferred_element_type=jnp.float32)
+
+    half = rows // 2
+    piece = half // pieces
+    cuts = [(p * piece, (p + 1) * piece) for p in range(pieces)]
+    for c in range(chunks - lag, chunks):
+        relay(c)
+    for role in (ACROSS_X, ACROSS_Y):
+        for c in range(chunks):
+            core[role, c].wait_recv()
+    pack(ACROSS_X)
+    pack(ACROSS_Y)
+    for copy in loads:
+        copy.wait()
+    swap = {ACROSS_X: expert(ACROSS_X)}
+    for c in range(chunks // 2):
+        relay_diagonal(c)
+    swap[ACROSS_Y] = expert(ACROSS_Y)
+    for c in range(chunks // 2, chunks):
+        relay_diagonal(c)
+
+    last_x, last_y, last_d = [], [], []
+
+    def post(buffer, landing, lo, hi, value, peer, sends):
+        buffer[lo:hi] = value.astype(jnp.bfloat16)
+        sends.append(link(buffer.at[pl.ds(lo, hi - lo)], landing, peer))
+
+    swap[ACROSS_X].wait_recv()
+    spread_x = spread(ACROSS_X)
+    for lo, hi in cuts:
+        land = from_x.at[pl.ds(lo, piece)]
+        post(to_x, land, lo, hi, unpack(ACROSS_X, spread_x, lo, hi), at_x, last_x)
+    swap[ACROSS_Y].wait_recv()
+    spread_y = spread(ACROSS_Y)
+    for lo, hi in cuts:
+        lo, hi = lo + half, hi + half
+        land = from_y.at[pl.ds(lo, piece)]
+        post(to_y, land, lo, hi, unpack(ACROSS_Y, spread_y, lo, hi), at_y, last_y)
+    for c in range(chunks):
+        core[DIAGONAL, c].wait_recv()
+    pack(DIAGONAL)
+    swap[DIAGONAL] = expert(DIAGONAL)
+    for c in range(chunks):
+        core[OWN, c].wait_recv()
+    pack(OWN)
+    swap[DIAGONAL].wait_recv()
+    spread_d = spread(DIAGONAL)
+    over_x, over_y = [], []
+    for lo, hi in cuts:
+        land = via_x.at[pl.ds(lo, piece)]
+        post(to_d, land, lo, hi, unpack(DIAGONAL, spread_d, lo, hi), at_x, over_x)
+        land = via_y.at[pl.ds(lo, piece)]
+        lo, hi = lo + half, hi + half
+        post(to_d, land, lo, hi, unpack(DIAGONAL, spread_d, lo, hi), at_y, over_y)
+    swap[OWN] = expert(OWN)
+    for p, (lo, hi) in enumerate(cuts):
+        over_x[p].wait_recv()
+        added = via_x[lo:hi].astype(jnp.float32)
+        land = from_y.at[pl.ds(lo, piece)]
+        post(to_y, land, lo, hi, unpack(ACROSS_Y, spread_y, lo, hi) + added, at_y, last_y)
+        over_y[p].wait_recv()
+        added = via_y[lo:hi].astype(jnp.float32)
+        lo, hi = lo + half, hi + half
+        land = from_x.at[pl.ds(lo, piece)]
+        post(to_x, land, lo, hi, unpack(ACROSS_X, spread_x, lo, hi) + added, at_x, last_x)
+    swap[OWN].wait_recv()
+    total[...] = unpack(OWN, spread(OWN), 0, rows) + tok[OWN, 0].astype(jnp.float32)
+    for p, (lo, hi) in enumerate(cuts):
+        last_x[p].wait_recv()
+        total[lo:hi] += from_x[lo:hi].astype(jnp.float32)
+        last_y[p].wait_recv()
+        total[lo + half : hi + half] += from_y[lo + half : hi + half].astype(jnp.float32)
+    for p, (lo, hi) in enumerate(cuts):
+        last_y[pieces + p].wait_recv()
+        done = total[lo:hi] + from_y[lo:hi].astype(jnp.float32)
+        out_ref[0, lo:hi] = done.astype(jnp.bfloat16)
+        last_x[pieces + p].wait_recv()
+        lo, hi = lo + half, hi + half
+        done = total[lo:hi] + from_x[lo:hi].astype(jnp.float32)
+        out_ref[0, lo:hi] = done.astype(jnp.bfloat16)
+    for copy in started:
+        copy.wait_send()
+
+
+def fused(incoming, expert_ids, gate_scores, gate_proj, up_proj, down_proj):
+    _, rows, features = incoming.shape
+    top, ff = expert_ids.shape[2], gate_proj.shape[2]
+    n_pp, n_tp, n_ep = (lax.axis_size(a) for a in ("pp", "tp", "ep"))
+    cap = min(rows, 2 * rows * top // (n_tp * n_ep))
+    chunks, pieces = 8, 2
+    routing = jnp.concatenate([expert_ids[0].astype(jnp.float32), gate_scores[0]], axis=1).T
+    routing = jnp.pad(routing, ((0, -2 * top % 8), (0, 0)))
+    hbm, vmem = pl.BlockSpec(memory_space=pl.ANY), pl.BlockSpec(memory_space=pltpu.VMEM)
+    narrow = functools.partial(pltpu.VMEM, dtype=jnp.bfloat16)
+    copies = 8 * chunks + 7 + 4 + 6 * pieces
+    return pl.pallas_call(
+        functools.partial(exchange_kernel, (n_pp, n_tp, n_ep, top, cap, chunks, pieces)),
+        out_shape=jax.ShapeDtypeStruct(incoming.shape, incoming.dtype),
+        in_specs=[hbm] * 5,
+        out_specs=vmem,
+        scratch_shapes=[
+            narrow((features, ff)),
+            narrow((features, ff)),
+            narrow((ff, features)),
+            narrow((4, 2, rows, features)),
+            pltpu.VMEM((8,) + routing.shape, jnp.float32),
+            narrow((4, 2 * cap, features)),
+            narrow((2 * cap, ff)),
+            narrow((4, cap, features)),
+            narrow((4, cap, features)),
+            narrow((4, cap, features)),
+            narrow((rows, features)),
+            narrow((rows, features)),
+            narrow((rows, features)),
+            narrow((rows, features)),
+            narrow((rows, features)),
+            narrow((rows // 2, features)),
+            narrow((rows // 2, features)),
+            pltpu.VMEM((rows, features), jnp.float32),
+            pltpu.SemaphoreType.DMA((copies,)),
+            pltpu.SemaphoreType.DMA((copies,)),
+            pltpu.SemaphoreType.DMA((4,)),
+        ],
+        compiler_params=pltpu.CompilerParams(collective_id=0, has_side_effects=True),
+    )(incoming, routing, gate_proj, up_proj, down_proj)
+
+
 def solution(mesh):
     placed = (
         P("pp", ("tp", "ep"), None),
@@ -71,6 +392,11 @@
         P(("tp", "ep"), None, None),
         P(("tp", "ep"), None, None),
     )
+    square = mesh.shape["tp"] == 4 and mesh.shape["ep"] == 2 and mesh.shape["pp"] > 1
     return jax.shard_map(
-        shards, mesh=mesh, in_specs=placed, out_specs=P("pp", ("tp", "ep"), None), check_vma=False
-    )
+        fused if square else shards,
+        mesh=mesh,
+        in_specs=placed,
+        out_specs=P("pp", ("tp", "ep"), None),
+        check_vma=False,
+    )

time: 118 us -> 58 us (0.49)
  waiting for transfers between devices: 55.7 us -> 0 us
  Pallas kernels: 0 us -> 54 us
  local copies, waits for them, and re-layouts: 21 us -> 2.48 us
  starting transfers between devices: 15.8 us -> 0 us
  matrix products: 13.7 us -> 0 us
  other arithmetic: 10.7 us -> 1.37 us
    pallas_call x0 -> x1, Pallas kernels: none -> 54 us  [fused(): pl.pallas_call(functools.partial(exchange_kernel, (n_pp, n_tp, n_ep, top,...]
    all_to_all x3 -> x0, waiting for transfers between devices: 51.7 us -> none  [the longest x1 25.9 us: shards(): lax.all_to_all(outgoing, ('tp', 'ep'), split_axis=0, concat_axis=0, tiled...]
    dot_general x2 -> x0, matrix products: 13.7 us -> none  [the longest x1 8.23 us: expert_apply(): jnp.dot(hidden, down_mat, preferred_element_type=jnp.float32)]
    all_to_all x3 -> x0, starting transfers between devices: 12.7 us -> none  [the longest x1 4.65 us: shards(): lax.all_to_all(answered, ('tp', 'ep'), split_axis=0, concat_axis=0, tiled...]
    gather x2 -> x0, local copies, waits for them, and re-layouts: 11.6 us -> none  [the longest x1 6.36 us: shards(): outgoing = with_blank[source_row].reshape(expert_count, capacity, features)]
    reduce_sum x4 -> x0, other arithmetic: 6.15 us -> none  [the longest x1 4.81 us: shards(): jnp.sum(weights[:, :, None] * picked.astype(jnp.float32), axis=1)]
    ppermute x1 -> x0, waiting for transfers between devices: 4.07 us -> none  [shifted(): return lax.ppermute(block, axis, route)]
    convert_element_type x2 -> x0, local copies, waits for them, and re-layouts: 3.48 us -> none  [the longest x1 3.39 us: shards(): picked.astype(jnp.float32)]
  transfers between devices with their start and end apart: 4 -> 0, of which waited for: 3 -> 0; matrix products, arithmetic and copies ran while one was open for 13% -> 0% of each run, Pallas kernels for 0% -> 0%
where the time goes in v1:
time: 58 us; the launch traced here: 57.8 us
  Pallas kernels  54 us (93%)
  local copies, waits for them, and re-layouts  2.48 us (4%)
  other arithmetic  1.37 us (2%)
    pallas_call x1, Pallas kernels, fused(): pl.pallas_call(functools.partial(exchange_kernel, (n_pp, n_tp, n_ep, top,...  54 us
    unnamed x1, local copies, waits for them, and re-layouts  1.88 us

profile of v1, /device:TPU:0, one launch (start us, length us, event | category | flops | bytes accessed | tf_op | source)
XLA Modules:
  0.0 57.8 jit_solution(5674653522609979337)
XLA Ops:
  0.0 0.7 %convert_bitcast_fusion = f32[128,2]{0,1:T(2,128)S(1)} fusion(s32[1,128,2]{1,2,0:T(2,128)} %param.7), kind=kLoop, calls=%fused_computation.1 | loop fusion | flops 256 | bytes 2048 | tf_op jit(solution)/shard_map/convert_element_type | solution.py:349
  0.7 0.7 %maximum_bitcast_fusion = f32[4,128]{1,0:T(4,128)S(1)} fusion(f32[128,2]{0,1:T(2,128)} %bitcast.5, f32[128,2]{0,1:T(2,128)S(1)} %convert_bitcast_fusion), kind=kLoop, calls=%fused_computation | loop fusion | flops 512 | bytes 4096 | tf_op jit(solution)/shard_map/transpose | solution.py:349
  1.4 0.6 %pad.4.routing = f32[8,128]{1,0:T(8,128)} pad(f32[4,128]{1,0:T(4,128)S(1)} %maximum_bitcast_fusion, f32[]{:T(128)} %constant.2.clone.1), padding=0_4x0_0 | pad | bytes 6148 | tf_op jit(solution)/shard_map/jit(_pad)/pad | solution.py:350
  2.0 54.0 %shard_map.64 = bf16[1,128,2048]{2,1,0:T(8,128)(2,1)} custom-call(bf16[1,128,2048]{2,1,0:T(8,128)(2,1)} %incoming.1, f32[8,128]{1,0:T(8,128)} %pad.4.routing, bf16[1,2048,768]{2,1,0:T(8,128)(2,1)} %gate_hbm.1, bf16[1,2048,768]{2,1,0:T(8,128)(2,1)} %up_hbm.1, bf16[1,768,2048]{2,1,0:T(8,128)(2,1)} %down_hbm.1), custom_call_target="tpu_custom_call" | custom-call | tf_op jit(solution)/shard_map/pallas_call | solution.py:354
  56.0 1.9 %copy.8 = bf16[1,128,2048]{2,1,0:T(8,128)(2,1)} copy(bf16[1,128,2048]{2,1,0:T(8,128)(2,1)} %shard_map.64) | data formatting | bytes 1048576

commit v2 on v1

--- a/solution.py
+++ b/solution.py
@@ -72,7 +72,8 @@
 def exchange_kernel(
     sizes,
     incoming,
-    routing,
+    ids_hbm,
+    scores_hbm,
     gate_hbm,
     up_hbm,
     down_hbm,
@@ -81,7 +82,8 @@
     up_w,
     down_w,
     tok,
-    meta,
+    meta_ids,
+    meta_scores,
     packed,
     hidden,
     kept,
@@ -109,16 +111,23 @@
     at_core = {"tp": other_core}
     ahead, behind = {"pp": (pp + 1) % n_pp}, {"pp": (pp + n_pp - 1) % n_pp}
 
-    loads = [
-        pltpu.make_async_copy(src.at[0], dst, load_sem.at[i])
-        for i, (src, dst) in enumerate(((gate_hbm, gate_w), (up_hbm, up_w), (down_hbm, down_w)))
+    splits = 3 * chunks
+    loads = []
+    for src, dst in ((gate_hbm, gate_w), (up_hbm, up_w), (down_hbm, down_w)):
+        depth = dst.shape[0] // chunks
+        for c in range(chunks):
+            cut = pl.ds(c * depth, depth)
+            loads.append(pltpu.make_async_copy(src.at[0, cut], dst.at[cut], load_sem.at[len(loads)]))
+    own_meta = [
+        pltpu.make_async_copy(ids_hbm, meta_ids.at[0], load_sem.at[splits]),
+        pltpu.make_async_copy(scores_hbm, meta_scores.at[0], load_sem.at[splits + 1]),
     ]
-    own_meta = pltpu.make_async_copy(routing, meta.at[0], load_sem.at[3])
 
     barrier = pltpu.get_barrier_semaphore()
     for peer in (at_x, at_y, at_core, ahead, behind):
         pl.semaphore_signal(barrier, inc=1, device_id=peer, device_id_type=MESH)
-    own_meta.start()
+    for copy in own_meta:
+        copy.start()
     pl.semaphore_wait(barrier, 5)
 
     started = []
@@ -144,12 +153,15 @@
         return tok.at[role, side, part[c]]
 
     hop = [link(incoming.at[0, part[c]], block(OWN, 0, c), ahead) for c in range(chunks)]
-    for copy in loads:
-        copy.start()
-    own_meta.wait()
-    meta_x = link(meta.at[0], meta.at[2], at_x)
-    meta_y = link(meta.at[0], meta.at[4], at_y)
-    meta_core = [link(meta.at[0], meta.at[1], at_core)]
+    for copy in own_meta:
+        copy.wait()
+
+    def meta_link(src, dst, peer):
+        return [link(m.at[src], m.at[dst], peer) for m in (meta_ids, meta_scores)]
+
+    meta_x = meta_link(0, 2, at_x)
+    meta_y = meta_link(0, 4, at_y)
+    meta_core = meta_link(0, 1, at_core)
     out_x, out_y, out_d, core = {}, {}, {}, {}
 
     def relay(c):
@@ -173,14 +185,19 @@
         out_y[c] = link(block(OWN, 0, c), block(ACROSS_Y, 0, c), at_y)
         core[OWN, c] = link(block(OWN, 0, c), block(OWN, 1, c), at_core)
         if c == 0:
-            meta_x.wait_recv()
-            meta_d = link(meta.at[2], meta.at[6], at_y)
-            meta_core.append(link(meta.at[2], meta.at[3], at_core))
-            meta_y.wait_recv()
-            meta_core.append(link(meta.at[4], meta.at[5], at_core))
+            for copy in meta_x:
+                copy.wait_recv()
+            meta_d = meta_link(2, 6, at_y)
+            meta_core += meta_link(2, 3, at_core)
+            for copy in meta_y:
+                copy.wait_recv()
+            meta_core += meta_link(4, 5, at_core)
         if c == 1:
-            meta_d.wait_recv()
-            meta_core.append(link(meta.at[6], meta.at[7], at_core))
+            for copy in meta_d:
+                copy.wait_recv()
+            meta_core += meta_link(6, 7, at_core)
+        for copy in loads[c::chunks]:
+            copy.start()
         if c >= lag:
             relay(c - lag)
     for copy in meta_core:
@@ -188,8 +205,8 @@
 
     lane = lax.broadcasted_iota(jnp.int32, (rows, rows), 1)
     earlier = (lax.broadcasted_iota(jnp.int32, (rows, rows), 0) < lane).astype(jnp.bfloat16)
-    ids = [meta[:, k, :] for k in range(top)]
-    scores = [meta[:, top + k, :] for k in range(top)]
+    ids = [meta_ids[:, k, :] for k in range(top)]
+    scores = [meta_scores[:, k, :] for k in range(top)]
     score_sum = functools.reduce(jnp.add, scores)
 
     def ranks(expert):
@@ -203,8 +220,8 @@
         score = sum(jnp.where(n, s, 0.0) for n, s in zip(named, scores))
         return jnp.where(any_named, before, -1.0), score / score_sum
 
-    mine = (tp * n_ep + ep).astype(jnp.float32)
-    theirs = (other_core * n_ep + ep).astype(jnp.float32)
+    mine = tp * n_ep + ep
+    theirs = other_core * n_ep + ep
     slot_mine, weight_mine = ranks(mine)
     slot_theirs, _ = ranks(theirs)
     slot_index = lax.broadcasted_iota(jnp.int32, (cap, rows), 0).astype(jnp.float32)
@@ -346,22 +363,21 @@
     n_pp, n_tp, n_ep = (lax.axis_size(a) for a in ("pp", "tp", "ep"))
     cap = min(rows, 2 * rows * top // (n_tp * n_ep))
     chunks, pieces = 8, 2
-    routing = jnp.concatenate([expert_ids[0].astype(jnp.float32), gate_scores[0]], axis=1).T
-    routing = jnp.pad(routing, ((0, -2 * top % 8), (0, 0)))
     hbm, vmem = pl.BlockSpec(memory_space=pl.ANY), pl.BlockSpec(memory_space=pltpu.VMEM)
     narrow = functools.partial(pltpu.VMEM, dtype=jnp.bfloat16)
-    copies = 8 * chunks + 7 + 4 + 6 * pieces
+    copies = 8 * chunks + 2 * 7 + 4 + 6 * pieces
     return pl.pallas_call(
         functools.partial(exchange_kernel, (n_pp, n_tp, n_ep, top, cap, chunks, pieces)),
-        out_shape=jax.ShapeDtypeStruct(incoming.shape, incoming.dtype),
-        in_specs=[hbm] * 5,
+        out_shape=pltpu.VMEM(incoming.shape, incoming.dtype),
+        in_specs=[hbm] * 6,
         out_specs=vmem,
         scratch_shapes=[
             narrow((features, ff)),
             narrow((features, ff)),
             narrow((ff, features)),
             narrow((4, 2, rows, features)),
-            pltpu.VMEM((8,) + routing.shape, jnp.float32),
+            pltpu.VMEM((8, top, rows), jnp.int32),
+            pltpu.VMEM((8, top, rows), jnp.float32),
             narrow((4, 2 * cap, features)),
             narrow((2 * cap, ff)),
             narrow((4, cap, features)),
@@ -377,10 +393,10 @@
             pltpu.VMEM((rows, features), jnp.float32),
             pltpu.SemaphoreType.DMA((copies,)),
             pltpu.SemaphoreType.DMA((copies,)),
-            pltpu.SemaphoreType.DMA((4,)),
+            pltpu.SemaphoreType.DMA((3 * chunks + 2,)),
         ],
         compiler_params=pltpu.CompilerParams(collective_id=0, has_side_effects=True),
-    )(incoming, routing, gate_proj, up_proj, down_proj)
+    )(incoming, expert_ids[0].T, gate_scores[0].T, gate_proj, up_proj, down_proj)
 
 
 def solution(mesh):

time: 58 us -> 54.5 us (0.940)
  local copies, waits for them, and re-layouts: 2.48 us -> 0.8 us
  other arithmetic: 1.37 us -> 0 us
    unnamed x1, local copies, waits for them, and re-layouts: 1.88 us -> 0.8 us
    transpose x1 -> x0, other arithmetic: 0.69 us -> none  [fused(): jnp.concatenate([expert_ids[0].astype(jnp.float32), gate_scores[0]], axis=1)]
    convert_element_type x1 -> x0, other arithmetic: 0.68 us -> none  [fused(): expert_ids[0].astype(jnp.float32)]
    pad x1 -> x0, local copies, waits for them, and re-layouts: 0.6 us -> none  [fused(): routing = jnp.pad(routing, ((0, -2 * top % 8), (0, 0)))]
where the time goes in v2:
time: 54.5 us; the launch traced here: 54.3 us
  Pallas kernels  53.5 us (98%)
  local copies, waits for them, and re-layouts  0.8 us (1%)
    pallas_call x1, Pallas kernels, fused(): pl.pallas_call(functools.partial(exchange_kernel, (n_pp, n_tp, n_ep, top,...  53.5 us

profile of v2, /device:TPU:0, one launch (start us, length us, event | category | flops | bytes accessed | tf_op | source)
XLA Modules:
  0.0 54.3 jit_solution(631195283482125665)
XLA Ops:
  0.0 53.5 %shard_map.64 = bf16[1,128,2048]{2,1,0:T(8,128)(2,1)S(1)} custom-call(bf16[1,128,2048]{2,1,0:T(8,128)(2,1)} %incoming.1, s32[2,128]{1,0:T(2,128)} %bitcast.6, f32[2,128]{1,0:T(2,128)} %bitcast.7, bf16[1,2048,768]{2,1,0:T(8,128)(2,1)} %gate_hbm.1, bf16[1,2048,768]{2,1,0:T(8,128)(2,1)} %up_hbm.1, bf16[1,768,2048]{2,1,0:T(8,128)(2,1)} %down_hbm.1), custom_call_target="tpu_custom_call" | custom-call | tf_op jit(solution)/shard_map/pallas_call | solution.py:369
  53.5 0.8 %copy.8 = bf16[1,128,2048]{2,1,0:T(8,128)(2,1)} copy(bf16[1,128,2048]{2,1,0:T(8,128)(2,1)S(1)} %shard_map.64) | data formatting | bytes 1048576

commit v3 on v2

--- a/solution.py
+++ b/solution.py
@@ -178,7 +178,7 @@
         out_d[c].wait_recv()
         core[DIAGONAL, c] = link(block(DIAGONAL, 0, c), block(DIAGONAL, 1, c), at_core)
 
-    lag = 2
+    lag = chunks
     for c in range(chunks):
         hop[c].wait_recv()
         out_x[c] = link(block(OWN, 0, c), block(ACROSS_X, 0, c), at_x)
@@ -192,7 +192,7 @@
             for copy in meta_y:
                 copy.wait_recv()
             meta_core += meta_link(4, 5, at_core)
-        if c == 1:
+        if c == chunks // 2:
             for copy in meta_d:
                 copy.wait_recv()
             meta_core += meta_link(6, 7, at_core)
@@ -288,10 +288,8 @@
     for copy in loads:
         copy.wait()
     swap = {ACROSS_X: expert(ACROSS_X)}
-    for c in range(chunks // 2):
-        relay_diagonal(c)
     swap[ACROSS_Y] = expert(ACROSS_Y)
-    for c in range(chunks // 2, chunks):
+    for c in range(chunks):
         relay_diagonal(c)
 
     last_x, last_y, last_d = [], [], []

time: 54.5 us -> 51 us (0.936)
  Pallas kernels: 53.5 us -> 50.1 us
    pallas_call x1, Pallas kernels: 53.5 us -> 50.1 us  [fused(): pl.pallas_call(functools.partial(exchange_kernel, (n_pp, n_tp, n_ep, top,...]
where the time goes in v3:
time: 51 us; the launch traced here: 50.9 us
  Pallas kernels  50.1 us (98%)
  local copies, waits for them, and re-layouts  0.8 us (2%)
    pallas_call x1, Pallas kernels, fused(): pl.pallas_call(functools.partial(exchange_kernel, (n_pp, n_tp, n_ep, top,...  50.1 us

profile of v3, /device:TPU:0, one launch (start us, length us, event | category | flops | bytes accessed | tf_op | source)
XLA Modules:
  0.0 50.9 jit_solution(15933087454570634944)
XLA Ops:
  0.0 50.1 %shard_map.64 = bf16[1,128,2048]{2,1,0:T(8,128)(2,1)S(1)} custom-call(bf16[1,128,2048]{2,1,0:T(8,128)(2,1)} %incoming.1, s32[2,128]{1,0:T(2,128)} %bitcast.6, f32[2,128]{1,0:T(2,128)} %bitcast.7, bf16[1,2048,768]{2,1,0:T(8,128)(2,1)} %gate_hbm.1, bf16[1,2048,768]{2,1,0:T(8,128)(2,1)} %up_hbm.1, bf16[1,768,2048]{2,1,0:T(8,128)(2,1)} %down_hbm.1), custom_call_target="tpu_custom_call" | custom-call | tf_op jit(solution)/shard_map/pallas_call | solution.py:367
  50.1 0.8 %copy.8 = bf16[1,128,2048]{2,1,0:T(8,128)(2,1)} copy(bf16[1,128,2048]{2,1,0:T(8,128)(2,1)S(1)} %shard_map.64) | data formatting | bytes 1048576
